TPU v7x, 256 devices: a 2x2x32 block of a 4x8x32 slice. The times are simulated.
256 devices in a mesh: groups: 4 (over x, y), seq: 32 (over z), head: 2 (over core).
Axes of the slice: x: 2, y: 2, z: 32, core: 2. Of those that a mesh axis runs over, the one named last changes fastest.
The devices are a block of a 4x8x32 slice.
Arguments:
- query_rows: bfloat16 [16384, 4096], P(('groups', 'seq'), 'head'), parts along dimension 0, may hold values from -160 to 160
- key_rows: bfloat16 [16384, 512], P(('groups', 'seq'), 'head'), parts along dimension 0, may hold values from -6 to 6
- value_rows: bfloat16 [16384, 512], P(('groups', 'seq'), 'head'), parts along dimension 0, may hold values from -6 to 6
- grad_out: bfloat16 [16384, 4096], P(('groups', 'seq'), 'head'), parts along dimension 0, may hold values from -6 to 6
- lengths: int32 [512], P(('groups', 'seq')), parts along dimension 0, may hold values from 1 to 2176, as said below
Outputs:
- attended: bfloat16 [16384, 4096], P(('groups', 'seq'), 'head'), parts along dimension 0
- grad_query: bfloat16 [16384, 4096], P(('groups', 'seq'), 'head'), parts along dimension 0
- grad_key: bfloat16 [16384, 512], P(('groups', 'seq'), 'head'), parts along dimension 0
- grad_value: bfloat16 [16384, 512], P(('groups', 'seq'), 'head'), parts along dimension 0
There are 4 independent parts, one for each index of `groups`. A program takes and returns all parts, laid end to end along the dimension named above; each array names one. Nothing has to cross between parts.
Inputs may be any that keep to these rules, and one draw needn't show every extreme that they name: The 128 lengths sum to 4096; the first document is the longest, with exactly 2176 tokens.
All inputs are finite; a program needn't handle non-finite values.
Results may differ from a plain program's by a relative error of at most 0.035.
Values may be sent and summed in bfloat16 or wider, within the bound.
No kernel may reach another device: no remote copies, remote signals or barrier semaphores. Data moves between devices by JAX's collectives and lax.ppermute only.
A program may use at most 64 MiB of HBM per device.

v0:
```python
import math

import jax
import jax.numpy as jnp
from jax import lax
from jax.sharding import PartitionSpec as P

HD = 128


NEGATIVE = -1e30


def in_order(tiles, dim):
    tiles = jnp.moveaxis(tiles, 0, dim)
    dims = tiles.shape
    return tiles.reshape(*dims[:dim], dims[dim] * dims[dim + 1], *dims[dim + 2 :])


def from_everyone(shard, axis):
    size = lax.axis_size(axis)
    return lax.all_to_all(
        jnp.broadcast_to(shard[None], (size, *shard.shape)), axis, 0, 0, tiled=True
    )


def gather_directly(shard, axis, dim):
    return in_order(from_everyone(shard, axis), dim)


def from_behind(value, axis, steps):
    count = lax.axis_size(axis)
    leading, last = (max(0, -steps), min(count, count - steps))
    return lax.ppermute(value, axis, [(source, source + steps) for source in range(leading, last)])


def from_behind_2(block, axis, distance):
    devices = range(lax.axis_size(axis))
    route = [((i - distance) % len(devices), i) for i in devices]
    return lax.ppermute(block, axis, route)


def doc_index(ends, positions):
    return jnp.sum((ends[None, :] <= positions[:, None]).astype(jnp.int32), axis=1)


def block_mask(ends, query_pos, query_docs, key_pos):
    key_docs = doc_index(ends, key_pos)
    return (
        (query_docs[:, None] == key_docs[None, :])
        & (key_pos[None, :] <= query_pos[:, None])
        & (key_pos[None, :] >= 0)
    )


def needed(ends, query_pos, query_docs, key_first, block):
    key_last = key_first + block - 1
    last_doc = jnp.sum((ends <= key_last).astype(jnp.int32))
    return (key_first <= query_pos[-1]) & (key_last >= 0) & (last_doc >= query_docs[0])


def tile_scores(query_four, key_block, scale):
    return scale * jnp.einsum(
        "tagd,kad->tagk", query_four, key_block, preferred_element_type=jnp.float32
    )


def forward_block(state, query_four, key_block, value_block, allowed, scale):
    rowmax, rowsum, accum = state
    scores = tile_scores(query_four, key_block, scale)
    allowed = allowed[:, None, None, :]
    masked = jnp.where(allowed, scores, NEGATIVE)
    new_max = jnp.maximum(rowmax, jnp.max(masked, axis=-1))
    expo = jnp.where(allowed, jnp.exp(masked - new_max[..., None]), 0.0)
    factor = jnp.exp(rowmax - new_max)
    rowsum = rowsum * factor + jnp.sum(expo, axis=-1)
    update = jnp.einsum(
        "tagk,kad->tagd", expo.astype(jnp.bfloat16), value_block, preferred_element_type=jnp.float32
    )
    accum = accum * factor[..., None] + update
    return (new_max, rowsum, accum)


def backward_block(back, key_block, value_block, allowed):
    query_four, grad_four, lse, delta, query_pos, query_docs, ends, scale = back
    scores = tile_scores(query_four, key_block, scale)
    allowed = allowed[:, None, None, :]
    masked = jnp.where(allowed, scores, NEGATIVE)
    prob = jnp.where(allowed, jnp.exp(masked - lse[..., None]), 0.0)
    value_part = jnp.einsum(
        "tagk,tagd->kad", prob.astype(jnp.bfloat16), grad_four, preferred_element_type=jnp.float32
    )
    dprob = jnp.einsum("tagd,kad->tagk", grad_four, value_block, preferred_element_type=jnp.float32)
    dscore = (prob * (dprob - delta[..., None])).astype(jnp.bfloat16)
    query_part = jnp.einsum("tagk,kad->tagd", dscore, key_block, preferred_element_type=jnp.float32)
    key_part = jnp.einsum("tagk,tagd->kad", dscore, query_four, preferred_element_type=jnp.float32)
    return (query_part, key_part, value_part)


def sweep_forward(state, pairs, first_pos, context, block):
    query_four, query_pos, query_docs, ends, scale = context
    count = pairs.shape[0] // block
    split = pairs.reshape((count, block) + pairs.shape[1:])

    def visit(carry, item):
        number, piece = item
        key_first = first_pos + number * block
        key_pos = key_first + jnp.arange(block, dtype=jnp.int32)

        def work(carry_in):
            allowed = block_mask(ends, query_pos, query_docs, key_pos)
            return forward_block(carry_in, query_four, piece[:, 0], piece[:, 1], allowed, scale)

        def unchanged(carry_in):
            return carry_in

        return (
            lax.cond(needed(ends, query_pos, query_docs, key_first, block), work, unchanged, carry),
            None,
        )

    state, _ = lax.scan(visit, state, (jnp.arange(count, dtype=jnp.int32), split))
    return state


def sweep_backward(query_acc, pairs, first_pos, back, block):
    query_pos = back[4]
    query_docs = back[5]
    ends = back[6]
    count = pairs.shape[0] // block
    split = pairs.reshape((count, block) + pairs.shape[1:])

    def visit(carry, item):
        number, piece = item
        key_first = first_pos + number * block
        key_pos = key_first + jnp.arange(block, dtype=jnp.int32)

        def work(carry_in):
            allowed = block_mask(ends, query_pos, query_docs, key_pos)
            query_part, key_part, value_part = backward_block(
                back, piece[:, 0], piece[:, 1], allowed
            )
            return (carry_in + query_part, jnp.stack([key_part, value_part], axis=1))

        def unchanged(carry_in):
            return (carry_in, jnp.zeros(piece.shape, jnp.float32))

        return lax.cond(
            needed(ends, query_pos, query_docs, key_first, block), work, unchanged, carry
        )

    query_acc, partial_grads = lax.scan(
        visit, query_acc, (jnp.arange(count, dtype=jnp.int32), split)
    )
    return (query_acc, partial_grads.reshape(pairs.shape))


def shards(query_rows, key_rows, value_rows, grad_out, lengths):
    tok = query_rows.shape[0]
    kv_heads = key_rows.shape[1] // HD
    q_heads = query_rows.shape[1] // HD
    group = q_heads // kv_heads
    scale = 1.0 / math.sqrt(HD)
    devices = lax.axis_size("seq")
    index = lax.axis_index("seq")
    reach = devices // 2 + 1
    every = gather_directly(lengths, "seq", 0)
    ends = jnp.cumsum(every)
    query_pos = index * tok + jnp.arange(tok, dtype=jnp.int32)
    query_docs = doc_index(ends, query_pos)
    query_four = query_rows.reshape(tok, kv_heads, group, HD)
    grad_four = grad_out.reshape(tok, kv_heads, group, HD)
    own_pairs = jnp.stack(
        [key_rows.reshape(tok, kv_heads, HD), value_rows.reshape(tok, kv_heads, HD)], axis=1
    )
    context = (query_four, query_pos, query_docs, ends, scale)
    start_state = (
        jnp.full((tok, kv_heads, group), NEGATIVE, jnp.float32),
        jnp.zeros((tok, kv_heads, group), jnp.float32),
        jnp.zeros((tok, kv_heads, group, HD), jnp.float32),
    )
    state = sweep_forward(start_state, own_pairs, index * tok, context, tok)

    def forward_turn(step, carry):
        state_in, moving = carry
        moving = from_behind(moving, "seq", 1)
        return (sweep_forward(state_in, moving, (index - step) * tok, context, tok), moving)

    state, _ = lax.fori_loop(1, reach + 1, forward_turn, (state, own_pairs))
    rowmax, rowsum, accum = state
    attended = (accum / rowsum[..., None]).astype(jnp.bfloat16)
    lse = rowmax + jnp.log(rowsum)
    delta = jnp.sum(grad_four.astype(jnp.float32) * attended.astype(jnp.float32), axis=-1)
    back = (query_four, grad_four, lse, delta, query_pos, query_docs, ends, scale)
    zero_query = jnp.zeros((tok, kv_heads, group, HD), jnp.float32)
    query_acc, own_grads = sweep_backward(zero_query, own_pairs, index * tok, back, tok)

    def backward_turn(step, carry):
        query_in, moving, grads = carry
        moving = from_behind(moving, "seq", 1)
        grads = from_behind_2(grads.astype(jnp.bfloat16), "seq", 1).astype(grads.dtype)
        query_out, fresh = sweep_backward(query_in, moving, (index - step) * tok, back, tok)
        return (query_out, moving, grads + fresh)

    query_acc, _, grads = lax.fori_loop(
        1, reach + 1, backward_turn, (query_acc, own_pairs, own_grads)
    )
    grads = from_behind_2(grads.astype(jnp.bfloat16), "seq", -reach).astype(grads.dtype)
    attended_out = attended.reshape(tok, q_heads * HD)
    query_out = (scale * query_acc).astype(jnp.bfloat16).reshape(tok, q_heads * HD)
    key_out = (scale * grads[:, 0]).astype(jnp.bfloat16).reshape(tok, kv_heads * HD)
    value_out = grads[:, 1].astype(jnp.bfloat16).reshape(tok, kv_heads * HD)
    return (attended_out, query_out, key_out, value_out)


def solution(mesh):
    return jax.shard_map(
        shards,
        mesh=mesh,
        in_specs=(
            P(("groups", "seq"), "head"),
            P(("groups", "seq"), "head"),
            P(("groups", "seq"), "head"),
            P(("groups", "seq"), "head"),
            P(("groups", "seq")),
        ),
        out_specs=(
            P(("groups", "seq"), "head"),
            P(("groups", "seq"), "head"),
            P(("groups", "seq"), "head"),
            P(("groups", "seq"), "head"),
        ),
        check_vma=False,
    )
```

profile of v0, /device:TPU:44, one launch (start us, length us, event | category | flops | bytes accessed | tf_op | source)
XLA Modules:
  0.0 488.0 jit_solution(3098370475202483611)
XLA Ops:
  2.0 32.7 %all-to-all-start = ((s32[32,1,4]{2,1,0:T(1,128)}), s32[32,1,4]{2,1,0:T(1,128)S(1)}, u32[]{:S(2)}, u32[]{:S(2)}) async-start(s32[32,1,4]{2,1,0:T(1,128)} %broadcast_in_dim.122), calls=%async_computation | async-start | bytes 32768 | tf_op jit(solution)/shard_map/all_to_all | solution.py:22
  40.9 15.3 %all-to-all-done = s32[32,1,4]{2,1,0:T(1,128)S(1)} async-done(((s32[32,1,4]{2,1,0:T(1,128)}), s32[32,1,4]{2,1,0:T(1,128)S(1)}, u32[]{:S(2)}, u32[]{:S(2)}) %all-to-all-start) | async-done | bytes 544 | tf_op jit(solution)/shard_map/all_to_all | solution.py:22
  59.4 4.5 conditional.4
  63.9 158.9 %while.85 = (s32[]{:T(128)}, f32[128,2,8]{0,2,1:T(8,128)S(1)}, f32[128,2,8]{0,2,1:T(8,128)S(1)}, f32[128,2,8,128]{3,0,2,1:T(8,128)S(1)}, bf16[128,2,2,128]{3,0,2...) while((s32[]{:T(128)}, f32[128,2,8]{0,2,1:T(8,128)S(1)}, ...), condition=%wide.region_15.16_spmd, body=%wide.region_8.15_spmd.sunk | while | flops 137220624 | bytes 6897951 | solution.py:189
  71.8 4.1 collective-permute-start
  107.9 4.9 collective-permute-start
  127.1 4.9 collective-permute-start
  164.6 4.0 collective-permute-start
  174.2 4.3 collective-permute-start
  184.0 4.6 collective-permute-start
  203.6 4.1 collective-permute-start
  213.2 4.1 collective-permute-start
  232.1 213.6 %while.86 = (s32[]{:T(128)}, f32[128,2,8,128]{3,0,2,1:T(8,128)S(1)}, bf16[128,2,2,128]{3,0,2,1:T(8,128)(2,1)S(1)}, bf16[128,2,2,128]{3,0,2,1:T(8,128)(2,1)S(1)},...) while((s32[]{:T(128)}, ...), condition=%wide.region_25.26_spmd, body=%wide.region_20.25_spmd.sunk | while | flops 338280960 | bytes 12343523 | solution.py:205
  264.6 5.1 %collective-permute-start.1 = (bf16[128,2,2,128]{3,0,2,1:T(8,128)(2,1)S(1)}, bf16[128,2,2,128]{3,0,2,1:T(8,128)(2,1)S(1)}, u32[]{:S(2)}, u32[]{:S(2)}) collective-permute-start(bf16[128,2,2,128]{3,0,2,1:T(8,128)(2,1)S(1)} %get-tuple-element.1470), channel_id=1, source_target_pairs={{0,2},{2,4},{4,6},{6,8},{8,10},{10,12},{12,14},{14,16},{16,18},{18... | collective-permute-start | bytes 393224 | tf_op jit(solution)/shard_map/while/body/eval_jaxpr/ppermute | solution.py:34
  276.9 5.6 %collective-permute-start.1 = (bf16[128,2,2,128]{3,0,2,1:T(8,128)(2,1)S(1)}, bf16[128,2,2,128]{3,0,2,1:T(8,128)(2,1)S(1)}, u32[]{:S(2)}, u32[]{:S(2)}) collective-permute-start(bf16[128,2,2,128]{3,0,2,1:T(8,128)(2,1)S(1)} %get-tuple-element.1470), channel_id=1, source_target_pairs={{0,2},{2,4},{4,6},{6,8},{8,10},{10,12},{12,14},{14,16},{16,18},{18... | collective-permute-start | bytes 393224 | tf_op jit(solution)/shard_map/while/body/eval_jaxpr/ppermute | solution.py:34
  301.8 4.3 collective-permute-start.1
  313.9 4.4 collective-permute-start.1
  359.8 5.4 %collective-permute-start.1 = (bf16[128,2,2,128]{3,0,2,1:T(8,128)(2,1)S(1)}, bf16[128,2,2,128]{3,0,2,1:T(8,128)(2,1)S(1)}, u32[]{:S(2)}, u32[]{:S(2)}) collective-permute-start(bf16[128,2,2,128]{3,0,2,1:T(8,128)(2,1)S(1)} %get-tuple-element.1470), channel_id=1, source_target_pairs={{0,2},{2,4},{4,6},{6,8},{8,10},{10,12},{12,14},{14,16},{16,18},{18... | collective-permute-start | bytes 393224 | tf_op jit(solution)/shard_map/while/body/eval_jaxpr/ppermute | solution.py:34
  373.3 4.5 collective-permute-start.1
  385.1 4.4 collective-permute-start.1
  417.5 13.6 %collective-permute-done.1 = bf16[128,2,2,128]{3,0,2,1:T(8,128)(2,1)S(1)} collective-permute-done((bf16[128,2,2,128]{3,0,2,1:T(8,128)(2,1)S(1)}, bf16[128,2,2,128]{3,0,2,1:T(8,128)(2,1)S(1)}, u32[]{:S(2)}, u32[]{:S(2)}) %collective-permute-start.1) | collective-permute-done | bytes 131104 | tf_op jit(solution)/shard_map/while/body/eval_jaxpr/ppermute | solution.py:34
  434.7 4.5 collective-permute-start.1
  445.7 34.3 %collective-permute-start.3 = (bf16[128,2,2,128]{3,0,2,1:T(8,128)(2,1)S(1)}, bf16[128,2,2,128]{3,0,2,1:T(8,128)(2,1)S(1)}, u32[]{:S(2)}, u32[]{:S(2)}) collective-permute-start(bf16[128,2,2,128]{3,0,2,1:T(8,128)(2,1)S(1)} %get-tuple-element.1056), channel_id=1, source_target_pairs={{34,0},{36,2},{38,4},{40,6},{42,8},{44,10},{46,12},{48,14},{50,16}... | collective-permute-start | bytes 393224 | tf_op jit(solution)/shard_map/ppermute | solution.py:40
  482.5 4.6 collective-permute-done.3
  (623 shorter events, 255.1 us)
Async XLA Ops:
  2.0 54.3 %all-to-all-start = ((s32[32,1,4]{2,1,0:T(1,128)}), s32[32,1,4]{2,1,0:T(1,128)S(1)}, u32[]{:S(2)}, u32[]{:S(2)}) async-start(s32[32,1,4]{2,1,0:T(1,128)} %broadcast_in_dim.122), calls=%async_computation | async-start | bytes 32768 | tf_op jit(solution)/shard_map/all_to_all | solution.py:22
  71.8 9.0 %collective-permute-start = (bf16[128,2,2,128]{3,0,2,1:T(8,128)(2,1)S(1)}, bf16[128,2,2,128]{3,0,2,1:T(8,128)(2,1)S(1)}, u32[]{:S(2)}, u32[]{:S(2)}) collective-permute-start(bf16[128,2,2,128]{3,0,2,1:T(8,128)(2,1)S(1)} %get-tuple-element.1424), channel_id=1, source_target_pairs={{0,2},{2,4},{4,6},{6,8},{8,10},{10,12},{12,14},{14,16},{16,18},{18... | collective-permute-start | bytes 393224 | tf_op jit(solution)/shard_map/while/body/eval_jaxpr/ppermute | solution.py:34
  107.9 9.7 %collective-permute-start = (bf16[128,2,2,128]{3,0,2,1:T(8,128)(2,1)S(1)}, bf16[128,2,2,128]{3,0,2,1:T(8,128)(2,1)S(1)}, u32[]{:S(2)}, u32[]{:S(2)}) collective-permute-start(bf16[128,2,2,128]{3,0,2,1:T(8,128)(2,1)S(1)} %get-tuple-element.1424), channel_id=1, source_target_pairs={{0,2},{2,4},{4,6},{6,8},{8,10},{10,12},{12,14},{14,16},{16,18},{18... | collective-permute-start | bytes 393224 | tf_op jit(solution)/shard_map/while/body/eval_jaxpr/ppermute | solution.py:34
  127.1 9.7 %collective-permute-start = (bf16[128,2,2,128]{3,0,2,1:T(8,128)(2,1)S(1)}, bf16[128,2,2,128]{3,0,2,1:T(8,128)(2,1)S(1)}, u32[]{:S(2)}, u32[]{:S(2)}) collective-permute-start(bf16[128,2,2,128]{3,0,2,1:T(8,128)(2,1)S(1)} %get-tuple-element.1424), channel_id=1, source_target_pairs={{0,2},{2,4},{4,6},{6,8},{8,10},{10,12},{12,14},{14,16},{16,18},{18... | collective-permute-start | bytes 393224 | tf_op jit(solution)/shard_map/while/body/eval_jaxpr/ppermute | solution.py:34
  164.6 8.8 %collective-permute-start = (bf16[128,2,2,128]{3,0,2,1:T(8,128)(2,1)S(1)}, bf16[128,2,2,128]{3,0,2,1:T(8,128)(2,1)S(1)}, u32[]{:S(2)}, u32[]{:S(2)}) collective-permute-start(bf16[128,2,2,128]{3,0,2,1:T(8,128)(2,1)S(1)} %get-tuple-element.1424), channel_id=1, source_target_pairs={{0,2},{2,4},{4,6},{6,8},{8,10},{10,12},{12,14},{14,16},{16,18},{18... | collective-permute-start | bytes 393224 | tf_op jit(solution)/shard_map/while/body/eval_jaxpr/ppermute | solution.py:34
  174.2 9.1 %collective-permute-start = (bf16[128,2,2,128]{3,0,2,1:T(8,128)(2,1)S(1)}, bf16[128,2,2,128]{3,0,2,1:T(8,128)(2,1)S(1)}, u32[]{:S(2)}, u32[]{:S(2)}) collective-permute-start(bf16[128,2,2,128]{3,0,2,1:T(8,128)(2,1)S(1)} %get-tuple-element.1424), channel_id=1, source_target_pairs={{0,2},{2,4},{4,6},{6,8},{8,10},{10,12},{12,14},{14,16},{16,18},{18... | collective-permute-start | bytes 393224 | tf_op jit(solution)/shard_map/while/body/eval_jaxpr/ppermute | solution.py:34
  184.0 9.5 %collective-permute-start = (bf16[128,2,2,128]{3,0,2,1:T(8,128)(2,1)S(1)}, bf16[128,2,2,128]{3,0,2,1:T(8,128)(2,1)S(1)}, u32[]{:S(2)}, u32[]{:S(2)}) collective-permute-start(bf16[128,2,2,128]{3,0,2,1:T(8,128)(2,1)S(1)} %get-tuple-element.1424), channel_id=1, source_target_pairs={{0,2},{2,4},{4,6},{6,8},{8,10},{10,12},{12,14},{14,16},{16,18},{18... | collective-permute-start | bytes 393224 | tf_op jit(solution)/shard_map/while/body/eval_jaxpr/ppermute | solution.py:34
  203.6 8.9 %collective-permute-start = (bf16[128,2,2,128]{3,0,2,1:T(8,128)(2,1)S(1)}, bf16[128,2,2,128]{3,0,2,1:T(8,128)(2,1)S(1)}, u32[]{:S(2)}, u32[]{:S(2)}) collective-permute-start(bf16[128,2,2,128]{3,0,2,1:T(8,128)(2,1)S(1)} %get-tuple-element.1424), channel_id=1, source_target_pairs={{0,2},{2,4},{4,6},{6,8},{8,10},{10,12},{12,14},{14,16},{16,18},{18... | collective-permute-start | bytes 393224 | tf_op jit(solution)/shard_map/while/body/eval_jaxpr/ppermute | solution.py:34
  213.2 9.0 %collective-permute-start = (bf16[128,2,2,128]{3,0,2,1:T(8,128)(2,1)S(1)}, bf16[128,2,2,128]{3,0,2,1:T(8,128)(2,1)S(1)}, u32[]{:S(2)}, u32[]{:S(2)}) collective-permute-start(bf16[128,2,2,128]{3,0,2,1:T(8,128)(2,1)S(1)} %get-tuple-element.1424), channel_id=1, source_target_pairs={{0,2},{2,4},{4,6},{6,8},{8,10},{10,12},{12,14},{14,16},{16,18},{18... | collective-permute-start | bytes 393224 | tf_op jit(solution)/shard_map/while/body/eval_jaxpr/ppermute | solution.py:34
  264.6 9.7 %collective-permute-start.1 = (bf16[128,2,2,128]{3,0,2,1:T(8,128)(2,1)S(1)}, bf16[128,2,2,128]{3,0,2,1:T(8,128)(2,1)S(1)}, u32[]{:S(2)}, u32[]{:S(2)}) collective-permute-start(bf16[128,2,2,128]{3,0,2,1:T(8,128)(2,1)S(1)} %get-tuple-element.1470), channel_id=1, source_target_pairs={{0,2},{2,4},{4,6},{6,8},{8,10},{10,12},{12,14},{14,16},{16,18},{18... | collective-permute-start | bytes 393224 | tf_op jit(solution)/shard_map/while/body/eval_jaxpr/ppermute | solution.py:34
  276.9 10.7 %collective-permute-start.1 = (bf16[128,2,2,128]{3,0,2,1:T(8,128)(2,1)S(1)}, bf16[128,2,2,128]{3,0,2,1:T(8,128)(2,1)S(1)}, u32[]{:S(2)}, u32[]{:S(2)}) collective-permute-start(bf16[128,2,2,128]{3,0,2,1:T(8,128)(2,1)S(1)} %get-tuple-element.1470), channel_id=1, source_target_pairs={{0,2},{2,4},{4,6},{6,8},{8,10},{10,12},{12,14},{14,16},{16,18},{18... | collective-permute-start | bytes 393224 | tf_op jit(solution)/shard_map/while/body/eval_jaxpr/ppermute | solution.py:34
  290.5 9.6 %collective-permute-start.1 = (bf16[128,2,2,128]{3,0,2,1:T(8,128)(2,1)S(1)}, bf16[128,2,2,128]{3,0,2,1:T(8,128)(2,1)S(1)}, u32[]{:S(2)}, u32[]{:S(2)}) collective-permute-start(bf16[128,2,2,128]{3,0,2,1:T(8,128)(2,1)S(1)} %get-tuple-element.1470), channel_id=1, source_target_pairs={{0,2},{2,4},{4,6},{6,8},{8,10},{10,12},{12,14},{14,16},{16,18},{18... | collective-permute-start | bytes 393224 | tf_op jit(solution)/shard_map/while/body/eval_jaxpr/ppermute | solution.py:34
  301.8 10.6 %collective-permute-start.1 = (bf16[128,2,2,128]{3,0,2,1:T(8,128)(2,1)S(1)}, bf16[128,2,2,128]{3,0,2,1:T(8,128)(2,1)S(1)}, u32[]{:S(2)}, u32[]{:S(2)}) collective-permute-start(bf16[128,2,2,128]{3,0,2,1:T(8,128)(2,1)S(1)} %get-tuple-element.1470), channel_id=1, source_target_pairs={{0,2},{2,4},{4,6},{6,8},{8,10},{10,12},{12,14},{14,16},{16,18},{18... | collective-permute-start | bytes 393224 | tf_op jit(solution)/shard_map/while/body/eval_jaxpr/ppermute | solution.py:34
  313.9 10.6 %collective-permute-start.1 = (bf16[128,2,2,128]{3,0,2,1:T(8,128)(2,1)S(1)}, bf16[128,2,2,128]{3,0,2,1:T(8,128)(2,1)S(1)}, u32[]{:S(2)}, u32[]{:S(2)}) collective-permute-start(bf16[128,2,2,128]{3,0,2,1:T(8,128)(2,1)S(1)} %get-tuple-element.1470), channel_id=1, source_target_pairs={{0,2},{2,4},{4,6},{6,8},{8,10},{10,12},{12,14},{14,16},{16,18},{18... | collective-permute-start | bytes 393224 | tf_op jit(solution)/shard_map/while/body/eval_jaxpr/ppermute | solution.py:34
  326.0 9.8 %collective-permute-start.1 = (bf16[128,2,2,128]{3,0,2,1:T(8,128)(2,1)S(1)}, bf16[128,2,2,128]{3,0,2,1:T(8,128)(2,1)S(1)}, u32[]{:S(2)}, u32[]{:S(2)}) collective-permute-start(bf16[128,2,2,128]{3,0,2,1:T(8,128)(2,1)S(1)} %get-tuple-element.1470), channel_id=1, source_target_pairs={{0,2},{2,4},{4,6},{6,8},{8,10},{10,12},{12,14},{14,16},{16,18},{18... | collective-permute-start | bytes 393224 | tf_op jit(solution)/shard_map/while/body/eval_jaxpr/ppermute | solution.py:34
  337.2 8.9 %collective-permute-start.1 = (bf16[128,2,2,128]{3,0,2,1:T(8,128)(2,1)S(1)}, bf16[128,2,2,128]{3,0,2,1:T(8,128)(2,1)S(1)}, u32[]{:S(2)}, u32[]{:S(2)}) collective-permute-start(bf16[128,2,2,128]{3,0,2,1:T(8,128)(2,1)S(1)} %get-tuple-element.1470), channel_id=1, source_target_pairs={{0,2},{2,4},{4,6},{6,8},{8,10},{10,12},{12,14},{14,16},{16,18},{18... | collective-permute-start | bytes 393224 | tf_op jit(solution)/shard_map/while/body/eval_jaxpr/ppermute | solution.py:34
  348.2 9.6 %collective-permute-start.1 = (bf16[128,2,2,128]{3,0,2,1:T(8,128)(2,1)S(1)}, bf16[128,2,2,128]{3,0,2,1:T(8,128)(2,1)S(1)}, u32[]{:S(2)}, u32[]{:S(2)}) collective-permute-start(bf16[128,2,2,128]{3,0,2,1:T(8,128)(2,1)S(1)} %get-tuple-element.1470), channel_id=1, source_target_pairs={{0,2},{2,4},{4,6},{6,8},{8,10},{10,12},{12,14},{14,16},{16,18},{18... | collective-permute-start | bytes 393224 | tf_op jit(solution)/shard_map/while/body/eval_jaxpr/ppermute | solution.py:34
  359.8 11.9 %collective-permute-start.1 = (bf16[128,2,2,128]{3,0,2,1:T(8,128)(2,1)S(1)}, bf16[128,2,2,128]{3,0,2,1:T(8,128)(2,1)S(1)}, u32[]{:S(2)}, u32[]{:S(2)}) collective-permute-start(bf16[128,2,2,128]{3,0,2,1:T(8,128)(2,1)S(1)} %get-tuple-element.1470), channel_id=1, source_target_pairs={{0,2},{2,4},{4,6},{6,8},{8,10},{10,12},{12,14},{14,16},{16,18},{18... | collective-permute-start | bytes 393224 | tf_op jit(solution)/shard_map/while/body/eval_jaxpr/ppermute | solution.py:34
  373.3 10.4 %collective-permute-start.1 = (bf16[128,2,2,128]{3,0,2,1:T(8,128)(2,1)S(1)}, bf16[128,2,2,128]{3,0,2,1:T(8,128)(2,1)S(1)}, u32[]{:S(2)}, u32[]{:S(2)}) collective-permute-start(bf16[128,2,2,128]{3,0,2,1:T(8,128)(2,1)S(1)} %get-tuple-element.1470), channel_id=1, source_target_pairs={{0,2},{2,4},{4,6},{6,8},{8,10},{10,12},{12,14},{14,16},{16,18},{18... | collective-permute-start | bytes 393224 | tf_op jit(solution)/shard_map/while/body/eval_jaxpr/ppermute | solution.py:34
  385.1 10.7 %collective-permute-start.1 = (bf16[128,2,2,128]{3,0,2,1:T(8,128)(2,1)S(1)}, bf16[128,2,2,128]{3,0,2,1:T(8,128)(2,1)S(1)}, u32[]{:S(2)}, u32[]{:S(2)}) collective-permute-start(bf16[128,2,2,128]{3,0,2,1:T(8,128)(2,1)S(1)} %get-tuple-element.1470), channel_id=1, source_target_pairs={{0,2},{2,4},{4,6},{6,8},{8,10},{10,12},{12,14},{14,16},{16,18},{18... | collective-permute-start | bytes 393224 | tf_op jit(solution)/shard_map/while/body/eval_jaxpr/ppermute | solution.py:34
  397.2 9.8 %collective-permute-start.1 = (bf16[128,2,2,128]{3,0,2,1:T(8,128)(2,1)S(1)}, bf16[128,2,2,128]{3,0,2,1:T(8,128)(2,1)S(1)}, u32[]{:S(2)}, u32[]{:S(2)}) collective-permute-start(bf16[128,2,2,128]{3,0,2,1:T(8,128)(2,1)S(1)} %get-tuple-element.1470), channel_id=1, source_target_pairs={{0,2},{2,4},{4,6},{6,8},{8,10},{10,12},{12,14},{14,16},{16,18},{18... | collective-permute-start | bytes 393224 | tf_op jit(solution)/shard_map/while/body/eval_jaxpr/ppermute | solution.py:34
  408.5 22.6 %collective-permute-start.1 = (bf16[128,2,2,128]{3,0,2,1:T(8,128)(2,1)S(1)}, bf16[128,2,2,128]{3,0,2,1:T(8,128)(2,1)S(1)}, u32[]{:S(2)}, u32[]{:S(2)}) collective-permute-start(bf16[128,2,2,128]{3,0,2,1:T(8,128)(2,1)S(1)} %get-tuple-element.1470), channel_id=1, source_target_pairs={{0,2},{2,4},{4,6},{6,8},{8,10},{10,12},{12,14},{14,16},{16,18},{18... | collective-permute-start | bytes 393224 | tf_op jit(solution)/shard_map/while/body/eval_jaxpr/ppermute | solution.py:34
  412.3 21.7 %collective-permute-start.2 = (bf16[128,2,2,128]{3,0,2,1:T(8,128)(2,1)}, bf16[128,2,2,128]{3,0,2,1:T(8,128)(2,1)S(1)}, u32[]{:S(2)}, u32[]{:S(2)}) collective-permute-start(bf16[128,2,2,128]{3,0,2,1:T(8,128)(2,1)} %copy-done.12), channel_id=1, source_target_pairs={{62,0},{0,2},{2,4},{4,6},{6,8},{8,10},{10,12},{12,14},{14,16},{16,... | collective-permute-start | bytes 393224 | tf_op jit(solution)/shard_map/while/body/eval_jaxpr/ppermute | solution.py:40
  445.7 41.4 %collective-permute-start.3 = (bf16[128,2,2,128]{3,0,2,1:T(8,128)(2,1)S(1)}, bf16[128,2,2,128]{3,0,2,1:T(8,128)(2,1)S(1)}, u32[]{:S(2)}, u32[]{:S(2)}) collective-permute-start(bf16[128,2,2,128]{3,0,2,1:T(8,128)(2,1)S(1)} %get-tuple-element.1056), channel_id=1, source_target_pairs={{34,0},{36,2},{38,4},{40,6},{42,8},{44,10},{46,12},{48,14},{50,16}... | collective-permute-start | bytes 393224 | tf_op jit(solution)/shard_map/ppermute | solution.py:40
  (169 other events, 395.6 us)
where the time goes:
time: 492 us; the launch traced here: 488 us
  starting transfers between devices  252 us (51%)
  local copies, waits for them, and re-layouts  92.8 us (19%)
  loops' own time  61 us (12%)
  waiting for transfers between devices  46.2 us (9%)
  other arithmetic  29.6 us (6%)
    ppermute x34, starting transfers between devices, from_behind(): lax.ppermute(value, axis, [(source, source + steps) for source in range(l...  134 us
    ppermute x18, starting transfers between devices, from_behind_2(): return lax.ppermute(block, axis, route)  84.9 us
    while x272, local copies, waits for them, and re-layouts  55.9 us
    another operation x1, loops' own time, shards(): state, _ = lax.fori_loop(1, reach + 1, forward_turn, (state, own_pairs))  36.9 us
    all_to_all x1, starting transfers between devices, from_everyone(): lax.all_to_all(jnp.broadcast_to(shard[None], (size, *shard.shape)), axis,...  32.7 us
    another operation x1, loops' own time, shards(): lax.fori_loop(1, reach + 1, backward_turn, (query_acc, own_pairs, own_gra...  23.7 us
    reduce_sum x35, other arithmetic, needed(): last_doc = jnp.sum((ends <= key_last).astype(jnp.int32))  23.5 us
    slice x35, local copies, waits for them, and re-layouts, needed(): query_pos[-1]  21.7 us
  transfers between devices with their start and end apart: 53, of which 12 were waited for; matrix products, arithmetic and copies ran while one was open for 10% of the time, Pallas kernels for 0%

commit v1 on v0

v1 whole, which is shorter than its diff:
```python
import functools
import math

import jax
import jax.numpy as jnp
from jax import lax
from jax.experimental import pallas as pl
from jax.experimental.pallas import tpu as pltpu
from jax.sharding import PartitionSpec as P

HD = 128
MOST = 2176
NEGATIVE = -1e30
SCALE = 1.0 / math.sqrt(HD)
LOG2E = math.log2(math.e)
C2 = SCALE * LOG2E

F32 = jnp.float32
BF16 = jnp.bfloat16

FORWARD_CALLS = ((0, 1, 2, 3, 4), (5, 6, 7, 8), (9, 10, 11, 12), (13, 14, 15), (16,))
BACKWARD_CALLS = ((16,), (15, 14), (13, 12, 11), (10, 9, 8), (7, 6, 5), (4, 3, 2), (1, 0))


def mm(a, b):
    return jnp.dot(a, b, preferred_element_type=F32)


def mm_tn(a, b):
    return lax.dot_general(a, b, (((0,), (0,)), ((), ())), preferred_element_type=F32)


def allowed_of(start, off, index, tok, shape):
    key = lax.broadcasted_iota(jnp.int32, shape, 0)
    keep = key >= start - (index - off) * tok
    if off == 0:
        query = lax.broadcasted_iota(jnp.int32, shape, 1) % tok
        keep = keep & (key <= query)
    return keep


def forward_kernel(offs, first, last, tok, group, *refs):
    count = len(offs)
    info, qt, start = refs[:3]
    kvs = refs[3 : 3 + count]
    rest = refs[3 + count :]
    if not first:
        m_in, l_in, acc_in = rest[:3]
        rest = rest[3:]
    if last:
        dot, att_out, lse_out, delta_out = rest[:4]
        m, l, acc = rest[4:]
    else:
        m, l, acc = rest
    index, reach = info[0], info[1]
    if first:
        m[0] = jnp.full(m.shape[1:], NEGATIVE, F32)
        l[0] = jnp.zeros(l.shape[1:], F32)
        acc[0] = jnp.zeros(acc.shape[1:], F32)
    else:
        m[0] = m_in[0]
        l[0] = l_in[0]
        acc[0] = acc_in[0]

    for off, kv in zip(offs, kvs):

        @pl.when(off <= reach)
        def _(off=off, kv=kv):
            scores = mm(kv[0, 0], qt[0])
            keep = allowed_of(start[...], off, index, tok, scores.shape)
            scores = jnp.where(keep, scores, NEGATIVE)
            old = m[0]
            new = jnp.maximum(old, jnp.max(scores, axis=0, keepdims=True))
            factor = jnp.exp2((old - new) * C2)
            expo = jnp.exp2((scores - new) * C2)
            m[0] = new
            l[0] = l[0] * factor + jnp.sum(expo, axis=0, keepdims=True)
            acc[0] = acc[0] * factor + mm_tn(kv[1, 0], expo.astype(BF16))

    if last:
        att = (acc[0] / l[0]).astype(BF16)
        lse_out[0] = m[0] * C2 + jnp.log2(l[0])
        wide = att.astype(F32)
        delta_out[0] = jnp.sum(wide * dot[0].astype(F32), axis=0, keepdims=True)
        for h in range(group):
            att_out[:, h * HD : (h + 1) * HD] = wide[:, h * tok : (h + 1) * tok].T.astype(BF16)


def backward_kernel(offs, first, last, tok, group, *refs):
    count = len(offs)
    info, qt, qn, dot, don, lse, delta, start = refs[:8]
    kvs = refs[8 : 8 + count]
    rest = refs[8 + count :]
    if not first:
        dq_in = rest[0]
        rest = rest[1:]
    outs = rest[:count]
    rest = rest[count:]
    if last:
        dq_out, dq = rest
    else:
        (dq,) = rest
    index, reach = info[0], info[1]
    if first:
        dq[0] = jnp.zeros(dq.shape[1:], F32)
    else:
        dq[0] = dq_in[0]

    for off, kv, out in zip(offs, kvs, outs):

        @pl.when(off <= reach)
        def _(off=off, kv=kv, out=out):
            scores = mm(kv[0, 0], qt[0])
            keep = allowed_of(start[...], off, index, tok, scores.shape)
            prob = jnp.exp2(jnp.where(keep, scores * C2 - lse[0], NEGATIVE))
            out[1, 0] = mm(prob.astype(BF16), don[0])
            dscore = (prob * (mm(kv[1, 0], dot[0]) - delta[0])).astype(BF16)
            out[0, 0] = mm(dscore, qn[0])
            dq[0] += mm_tn(kv[0, 0], dscore)

        @pl.when(off > reach)
        def _(out=out):
            out[...] = jnp.zeros(out.shape, F32)

    if last:
        total = dq[0] * SCALE
        for h in range(group):
            dq_out[:, h * HD : (h + 1) * HD] = total[:, h * tok : (h + 1) * tok].T.astype(BF16)


def by_head(*shape):
    zeros = (0,) * (len(shape) - 1)
    return pl.BlockSpec((1, *shape[1:]), lambda g, info: (g, *zeros))


def forward(offs, first, last, tok, info, qt, start, kvs, state, dot):
    kv_heads, _, wide = qt.shape
    group = wide // tok
    row = by_head(kv_heads, 1, wide)
    square = by_head(kv_heads, HD, wide)
    kv_spec = pl.BlockSpec((2, 1, tok, HD), lambda g, info: (0, g, 0, 0))
    in_specs = [square, pl.BlockSpec((1, wide), lambda g, info: (0, 0))] + [kv_spec] * len(kvs)
    args = [qt, start, *kvs]
    row_shape = jax.ShapeDtypeStruct((kv_heads, 1, wide), F32)
    square_shape = jax.ShapeDtypeStruct((kv_heads, HD, wide), F32)
    if not first:
        in_specs += [row, row, square]
        args += list(state)
    scratch = []
    if last:
        in_specs.append(square)
        args.append(dot)
        out_specs = [pl.BlockSpec((tok, group * HD), lambda g, info: (0, g)), row, row]
        out_shape = [jax.ShapeDtypeStruct((tok, kv_heads * group * HD), BF16), row_shape, row_shape]
        scratch = [pltpu.VMEM((1, 1, wide), F32), pltpu.VMEM((1, 1, wide), F32), pltpu.VMEM((1, HD, wide), F32)]
    else:
        out_specs = [row, row, square]
        out_shape = [row_shape, row_shape, square_shape]
    return pl.pallas_call(
        functools.partial(forward_kernel, offs, first, last, tok, group),
        out_shape=out_shape,
        grid_spec=pltpu.PrefetchScalarGridSpec(
            num_scalar_prefetch=1,
            grid=(kv_heads,),
            in_specs=in_specs,
            out_specs=out_specs,
            scratch_shapes=scratch,
        ),
        compiler_params=pltpu.CompilerParams(dimension_semantics=("arbitrary",)),
        cost_estimate=pl.CostEstimate(
            flops=4 * len(offs) * kv_heads * tok * wide * HD,
            transcendentals=len(offs) * kv_heads * tok * wide,
            bytes_accessed=8 * kv_heads * HD * wide,
        ),
        name="forward",
    )(info, *args)


def backward(offs, first, last, tok, info, qt, qn, dot, don, lse, delta, start, kvs, dq):
    kv_heads, _, wide = qt.shape
    group = wide // tok
    row = by_head(kv_heads, 1, wide)
    square = by_head(kv_heads, HD, wide)
    tall = by_head(kv_heads, wide, HD)
    kv_spec = pl.BlockSpec((2, 1, tok, HD), lambda g, info: (0, g, 0, 0))
    in_specs = [square, tall, square, tall, row, row, pl.BlockSpec((1, wide), lambda g, info: (0, 0))]
    in_specs += [kv_spec] * len(kvs)
    args = [qt, qn, dot, don, lse, delta, start, *kvs]
    if not first:
        in_specs.append(square)
        args.append(dq)
    out_specs = [kv_spec] * len(kvs)
    out_shape = [jax.ShapeDtypeStruct((2, kv_heads, tok, HD), F32)] * len(kvs)
    scratch = []
    if last:
        out_specs.append(pl.BlockSpec((tok, group * HD), lambda g, info: (0, g)))
        out_shape.append(jax.ShapeDtypeStruct((tok, kv_heads * group * HD), BF16))
        scratch = [pltpu.VMEM((1, HD, wide), F32)]
    else:
        out_specs.append(square)
        out_shape.append(jax.ShapeDtypeStruct((kv_heads, HD, wide), F32))
    return pl.pallas_call(
        functools.partial(backward_kernel, offs, first, last, tok, group),
        out_shape=out_shape,
        grid_spec=pltpu.PrefetchScalarGridSpec(
            num_scalar_prefetch=1,
            grid=(kv_heads,),
            in_specs=in_specs,
            out_specs=out_specs,
            scratch_shapes=scratch,
        ),
        compiler_params=pltpu.CompilerParams(dimension_semantics=("arbitrary",)),
        cost_estimate=pl.CostEstimate(
            flops=10 * len(offs) * kv_heads * tok * wide * HD,
            transcendentals=len(offs) * kv_heads * tok * wide,
            bytes_accessed=12 * kv_heads * HD * wide,
        ),
        name="backward",
    )(info, *args)


def calls(wanted, reach, down):
    kept = [tuple(o for o in offs if o <= reach) for offs in wanted]
    kept = [offs for offs in kept if offs]
    held = sorted(o for offs in kept for o in offs)
    extra = [(o,) for o in range(reach + 1) if o not in held]
    return extra[::-1] + kept if down else kept + extra


def start_of_documents(lengths, tok, index):
    devices = lax.axis_size("seq")
    have = lengths[None]
    while have.shape[0] < devices:
        held = have.shape[0]
        take = min(held, devices - held)
        route = [(i, (i + held) % devices) for i in range(devices)]
        have = jnp.concatenate([have, lax.ppermute(have[:take], "seq", route)])
    each = lengths.shape[0]
    owner = (index - jnp.arange(devices, dtype=jnp.int32)) % devices
    number = (owner[:, None] * each + jnp.arange(each, dtype=jnp.int32)[None]).reshape(-1)
    flat = have.reshape(-1)
    ends = jnp.sum(jnp.where(number[None] <= number[:, None], flat[None], 0), axis=1)
    position = index * tok + jnp.arange(tok, dtype=jnp.int32)
    return jnp.max(jnp.where(ends[None] <= position[:, None], ends[None], 0), axis=1)


def shards(query_rows, key_rows, value_rows, grad_out, lengths):
    tok = query_rows.shape[0]
    kv_heads = key_rows.shape[1] // HD
    q_heads = query_rows.shape[1] // HD
    group = q_heads // kv_heads
    wide = group * tok
    devices = lax.axis_size("seq")
    index = lax.axis_index("seq")
    assert MOST % tok == 0
    edge = MOST // tok
    reach = max(edge, devices - edge) - 1
    up = [(i, i + 1) for i in range(devices - 1) if i + 1 != edge]
    down = [(i + 1, i) for i in range(devices - 1) if i + 1 != edge]

    def heads_apart(rows):
        return rows.reshape(tok, kv_heads, HD).transpose(1, 0, 2)

    def heads_together(blocks):
        return blocks.transpose(1, 0, 2).reshape(tok, kv_heads * HD)

    block = jnp.stack([heads_apart(key_rows), heads_apart(value_rows)])
    blocks = [block]
    for _ in range(reach):
        blocks.append(lax.ppermute(blocks[-1], "seq", up))

    starts = start_of_documents(lengths, tok, index)
    middle = reach // 2
    starts, blocks[middle] = lax.optimization_barrier((starts, blocks[middle]))
    for k in range(middle + 1, reach + 1):
        blocks[k] = lax.ppermute(blocks[k - 1], "seq", up)
    back = index - starts[0] // tok
    info = jnp.stack([index, back]).astype(jnp.int32)
    start = jnp.tile(starts[None], (1, group))

    four = query_rows.reshape(tok, kv_heads, group, HD)
    grad_four = grad_out.reshape(tok, kv_heads, group, HD)
    qt = four.transpose(1, 3, 2, 0).reshape(kv_heads, HD, wide)
    qn = four.transpose(1, 2, 0, 3).reshape(kv_heads, wide, HD)
    dot = grad_four.transpose(1, 3, 2, 0).reshape(kv_heads, HD, wide)
    don = grad_four.transpose(1, 2, 0, 3).reshape(kv_heads, wide, HD)

    groups = calls(FORWARD_CALLS, reach, False)
    state = None
    for n, offs in enumerate(groups):
        state = forward(
            offs, n == 0, n == len(groups) - 1, tok, info, qt, start, [blocks[o] for o in offs], state, dot
        )
    attended, lse, delta = state

    groups = calls(BACKWARD_CALLS, reach, True)
    dq = None
    moving = None
    for n, offs in enumerate(groups):
        *fresh, dq = backward(
            offs, n == 0, n == len(groups) - 1, tok, info, qt, qn, dot, don, lse, delta, start,
            [blocks[o] for o in offs], dq,
        )
        for off, own in zip(offs, fresh):
            total = own if moving is None else own + moving.astype(F32)
            if off:
                moving = lax.ppermute(total.astype(BF16), "seq", down)
    key_out = heads_together((total[0] * SCALE).astype(BF16))
    value_out = heads_together(total[1].astype(BF16))
    return attended, dq, key_out, value_out


def solution(mesh):
    rows = P(("groups", "seq"), "head")
    return jax.shard_map(
        shards,
        mesh=mesh,
        in_specs=(rows, rows, rows, rows, P(("groups", "seq"))),
        out_specs=(rows, rows, rows, rows),
        check_vma=False,
    )
```

time: 492 us -> 345 us (0.70)
  the two profiles are of different devices: /device:TPU:44 before, /device:TPU:494 now
where the time goes in v1:
time: 345 us; the launch traced here: 344 us
  starting transfers between devices  151 us (44%)
  waiting for transfers between devices  112 us (32%)
  Pallas kernels  58.1 us (17%)
  local copies, waits for them, and re-layouts  12 us (3%)
  other arithmetic  8.56 us (2%)
    ppermute x16, waiting for transfers between devices, shards(): moving = lax.ppermute(total.astype(BF16), 'seq', down)  73.8 us
    ppermute x8, starting transfers between devices, shards(): blocks.append(lax.ppermute(blocks[-1], 'seq', up))  43.2 us
    ppermute x8, starting transfers between devices, shards(): blocks[k] = lax.ppermute(blocks[k - 1], 'seq', up)  37.7 us
    ppermute x5, starting transfers between devices, start_of_documents(): have = jnp.concatenate([have, lax.ppermute(have[:take], 'seq', route)])  37.6 us
    pallas_call x7, Pallas kernels, backward(): pl.pallas_call(functools.partial(backward_kernel, offs, first, last, tok,...  34.8 us
    ppermute x16, starting transfers between devices, shards(): moving = lax.ppermute(total.astype(BF16), 'seq', down)  33 us
    pallas_call x5, Pallas kernels, forward(): pl.pallas_call(functools.partial(forward_kernel, offs, first, last, tok,...  23.4 us
    ppermute x8, waiting for transfers between devices, shards(): blocks.append(lax.ppermute(blocks[-1], 'seq', up))  14.6 us
  transfers between devices with their start and end apart: 37, of which 27 were waited for; matrix products, arithmetic and copies ran while one was open for 2% of the time, Pallas kernels for 15%

profile of v1, /device:TPU:494, one launch (start us, length us, event | category | flops | bytes accessed | tf_op | source)
XLA Modules:
  0.0 343.5 jit_solution(8682775666472622762)
XLA Ops:
  11.1 5.6 %collective-permute-start.6 = (bf16[2,2,128,128]{3,2,1,0:T(8,128)(2,1)S(1)}, bf16[2,2,128,128]{3,2,1,0:T(8,128)(2,1)S(1)}, u32[]{:S(2)}, u32[]{:S(2)}) collective-permute-start(bf16[2,2,128,128]{3,2,1,0:T(8,128)(2,1)S(1)} %collective-permute-done.5.refs_4_.refs_8_), channel_id=1, source_target_pairs={{0,2},{2,4},{4,6},{6,8},{8,10},{10,12},{12,14},{14,16},{16,18},{18... | collective-permute-start | bytes 393224 | tf_op jit(solution)/shard_map/ppermute | solution.py:270
  53.8 8.1 %collective-permute-start.2 = (s32[4,4]{1,0:T(4,128)S(1)}, s32[4,4]{1,0:T(4,128)S(1)}, u32[]{:S(2)}, u32[]{:S(2)}) collective-permute-start(s32[4,4]{1,0:T(4,128)S(1)} %pad_add_fusion.1), channel_id=1, source_target_pairs={{0,8},{2,10},{4,12},{6,14},{8,16},{10,18},{12,20},{14,22},{16,24},... | collective-permute-start | bytes 200 | tf_op jit(solution)/shard_map/ppermute | solution.py:237
  66.1 10.8 %collective-permute-start.3 = (s32[8,4]{1,0:T(8,128)S(1)}, s32[8,4]{1,0:T(8,128)S(1)}, u32[]{:S(2)}, u32[]{:S(2)}) collective-permute-start(s32[8,4]{1,0:T(8,128)S(1)} %pad_add_fusion), channel_id=1, source_target_pairs={{0,16},{2,18},{4,20},{6,22},{8,24},{10,26},{12,28},{14,30},{16,32}... | collective-permute-start | bytes 392 | tf_op jit(solution)/shard_map/ppermute | solution.py:237
  78.7 16.0 %collective-permute-start.4 = (s32[16,4]{0,1:T(4,128)S(1)}, s32[16,4]{0,1:T(4,128)S(1)}, u32[]{:S(2)}, u32[]{:S(2)}) collective-permute-start(s32[16,4]{0,1:T(4,128)S(1)} %concatenate.22), channel_id=1, source_target_pairs={{0,32},{2,34},{4,36},{6,38},{8,40},{10,42},{12,44},{14,46},{16,48}... | collective-permute-start | bytes 776 | tf_op jit(solution)/shard_map/ppermute | solution.py:237
  94.8 5.9 %collective-permute-done.4 = s32[16,4]{0,1:T(4,128)S(1)} collective-permute-done((s32[16,4]{0,1:T(4,128)S(1)}, s32[16,4]{0,1:T(4,128)S(1)}, u32[]{:S(2)}, u32[]{:S(2)}) %collective-permute-start.4) | collective-permute-done | bytes 288 | tf_op jit(solution)/shard_map/ppermute | solution.py:237
  101.0 5.6 %collective-permute-start.12 = (bf16[2,2,128,128]{3,2,1,0:T(8,128)(2,1)S(1)}, bf16[2,2,128,128]{3,2,1,0:T(8,128)(2,1)S(1)}, u32[]{:S(2)}, u32[]{:S(2)}) collective-permute-start(bf16[2,2,128,128]{3,2,1,0:T(8,128)(2,1)S(1)} %collective-permute-done.11.refs_5_.refs_8_), channel_id=1, source_target_pairs={{0,2},{2,4},{4,6},{6,8},{8,10},{10,12},{12,14},{14,16},{16,18},{18... | collective-permute-start | bytes 393224 | tf_op jit(solution)/shard_map/ppermute | solution.py:270
  125.4 5.6 %collective-permute-start.15 = (bf16[2,2,128,128]{3,2,1,0:T(8,128)(2,1)S(1)}, bf16[2,2,128,128]{3,2,1,0:T(8,128)(2,1)S(1)}, u32[]{:S(2)}, u32[]{:S(2)}) collective-permute-start(bf16[2,2,128,128]{3,2,1,0:T(8,128)(2,1)S(1)} %collective-permute-done.14.refs_4_.refs_8_), channel_id=1, source_target_pairs={{0,2},{2,4},{4,6},{6,8},{8,10},{10,12},{12,14},{14,16},{16,18},{18... | collective-permute-start | bytes 393224 | tf_op jit(solution)/shard_map/ppermute | solution.py:276
  134.7 5.6 %collective-permute-start.16 = (bf16[2,2,128,128]{3,2,1,0:T(8,128)(2,1)S(1)}, bf16[2,2,128,128]{3,2,1,0:T(8,128)(2,1)S(1)}, u32[]{:S(2)}, u32[]{:S(2)}) collective-permute-start(bf16[2,2,128,128]{3,2,1,0:T(8,128)(2,1)S(1)} %collective-permute-done.15.refs_5_.refs_10_), channel_id=1, source_target_pairs={{0,2},{2,4},{4,6},{6,8},{8,10},{10,12},{12,14},{14,16},{16,18},{18... | collective-permute-start | bytes 393224 | tf_op jit(solution)/shard_map/ppermute | solution.py:276
  143.3 5.6 %collective-permute-start.17 = (bf16[2,2,128,128]{3,2,1,0:T(8,128)(2,1)S(1)}, bf16[2,2,128,128]{3,2,1,0:T(8,128)(2,1)S(1)}, u32[]{:S(2)}, u32[]{:S(2)}) collective-permute-start(bf16[2,2,128,128]{3,2,1,0:T(8,128)(2,1)S(1)} %collective-permute-done.16.refs_6_.refs_9_), channel_id=1, source_target_pairs={{0,2},{2,4},{4,6},{6,8},{8,10},{10,12},{12,14},{14,16},{16,18},{18... | collective-permute-start | bytes 393224 | tf_op jit(solution)/shard_map/ppermute | solution.py:276
  166.4 7.9 %forward.5 = (f32[2,1,1024]{2,1,0:T(1,128)}, f32[2,1,1024]{2,1,0:T(1,128)}, f32[2,128,1024]{2,1,0:T(8,128)}) custom-call(s32[2]{0:T(128)} %pad_add_fusion.3.refs_0_, bf16[2,128,1024]{2,1,0:T(8,128)(2,1)} %reshape.101.refs_1_, s32[1,1024]{1,0:T(1,128)} %bitcast.64, bf16[2,2,128,128]{3,2,1,0:T(8,128)(2,1)} %copy-done.3, bf16[2,2,128,128]{3,2,1,0:T(8,128)(2,1)} %copy-done.16, ...), custom_call_target="tpu_custom_call" | custom-call | flops 671088640 | bytes 2097152 | tf_op jit(solution)/shard_map/forward/pallas_call | solution.py:159
  176.4 6.0 %forward.6 = (f32[2,1,1024]{2,1,0:T(1,128)}, f32[2,1,1024]{2,1,0:T(1,128)}, f32[2,128,1024]{2,1,0:T(8,128)}) custom-call(s32[2]{0:T(128)} %pad_add_fusion.3.refs_0_, bf16[2,128,1024]{2,1,0:T(8,128)(2,1)} %reshape.101.refs_1_, s32[1,1024]{1,0:T(1,128)} %bitcast.65, bf16[2,2,128,128]{3,2,1,0:T(8,128)(2,1)} %copy-done.17, bf16[2,2,128,128]{3,2,1,0:T(8,128)(2,1)} %copy-done.18, ...), custom_call_target="tpu_custom_call" | custom-call | flops 536870912 | bytes 2097152 | tf_op jit(solution)/shard_map/forward/pallas_call | solution.py:159
  208.8 7.3 %collective-permute-done.22 = bf16[2,2,128,128]{3,2,1,0:T(8,128)(2,1)S(1)} collective-permute-done((bf16[2,2,128,128]{3,2,1,0:T(8,128)(2,1)S(1)}, bf16[2,2,128,128]{3,2,1,0:T(8,128)(2,1)S(1)}, u32[]{:S(2)}, u32[]{:S(2)}) %collective-permute-start.22) | collective-permute-done | bytes 131104 | tf_op jit(solution)/shard_map/ppermute | solution.py:307
  227.3 6.8 %collective-permute-done.24 = bf16[2,2,128,128]{3,2,1,0:T(8,128)(2,1)S(1)} collective-permute-done((bf16[2,2,128,128]{3,2,1,0:T(8,128)(2,1)S(1)}, bf16[2,2,128,128]{3,2,1,0:T(8,128)(2,1)S(1)}, u32[]{:S(2)}, u32[]{:S(2)}) %collective-permute-start.24) | collective-permute-done | bytes 131104 | tf_op jit(solution)/shard_map/ppermute | solution.py:307
  236.2 7.2 %collective-permute-done.25 = bf16[2,2,128,128]{3,2,1,0:T(8,128)(2,1)S(1)} collective-permute-done((bf16[2,2,128,128]{3,2,1,0:T(8,128)(2,1)S(1)}, bf16[2,2,128,128]{3,2,1,0:T(8,128)(2,1)S(1)}, u32[]{:S(2)}, u32[]{:S(2)}) %collective-permute-start.25) | collective-permute-done | bytes 131104 | tf_op jit(solution)/shard_map/ppermute | solution.py:307
  254.6 7.5 %collective-permute-done.27 = bf16[2,2,128,128]{3,2,1,0:T(8,128)(2,1)S(1)} collective-permute-done((bf16[2,2,128,128]{3,2,1,0:T(8,128)(2,1)S(1)}, bf16[2,2,128,128]{3,2,1,0:T(8,128)(2,1)S(1)}, u32[]{:S(2)}, u32[]{:S(2)}) %collective-permute-start.27) | collective-permute-done | bytes 131104 | tf_op jit(solution)/shard_map/ppermute | solution.py:307
  264.3 6.6 %collective-permute-done.28 = bf16[2,2,128,128]{3,2,1,0:T(8,128)(2,1)S(1)} collective-permute-done((bf16[2,2,128,128]{3,2,1,0:T(8,128)(2,1)S(1)}, bf16[2,2,128,128]{3,2,1,0:T(8,128)(2,1)S(1)}, u32[]{:S(2)}, u32[]{:S(2)}) %collective-permute-start.28) | collective-permute-done | bytes 131104 | tf_op jit(solution)/shard_map/ppermute | solution.py:307
  273.1 7.2 %backward.11 = (f32[2,2,128,128]{3,2,1,0:T(8,128)}, f32[2,2,128,128]{3,2,1,0:T(8,128)}, f32[2,2,128,128]{3,2,1,0:T(8,128)}, f32[2,128,1024]{2,1,0:T(8,128)}) custom-call(s32[2]{0:T(128)} %pad_add_fusion.3.refs_0_, bf16[2,128,1024]{2,1,0:T(8,128)(2,1)} %reshape.101.refs_1_, bf16[2,1024,128]{2,1,0:T(8,128)(2,1)} %bitcast.46, ...), custom_call_target="tpu_custom_call" | custom-call | flops 1006632960 | bytes 3145728 | tf_op jit(solution)/shard_map/backward/pallas_call | solution.py:202
  283.4 6.1 %collective-permute-done.30 = bf16[2,2,128,128]{3,2,1,0:T(8,128)(2,1)S(1)} collective-permute-done((bf16[2,2,128,128]{3,2,1,0:T(8,128)(2,1)S(1)}, bf16[2,2,128,128]{3,2,1,0:T(8,128)(2,1)S(1)}, u32[]{:S(2)}, u32[]{:S(2)}) %collective-permute-start.30) | collective-permute-done | bytes 131104 | tf_op jit(solution)/shard_map/ppermute | solution.py:307
  291.6 6.1 %collective-permute-done.31 = bf16[2,2,128,128]{3,2,1,0:T(8,128)(2,1)S(1)} collective-permute-done((bf16[2,2,128,128]{3,2,1,0:T(8,128)(2,1)S(1)}, bf16[2,2,128,128]{3,2,1,0:T(8,128)(2,1)S(1)}, u32[]{:S(2)}, u32[]{:S(2)}) %collective-permute-start.31) | collective-permute-done | bytes 131104 | tf_op jit(solution)/shard_map/ppermute | solution.py:307
  299.8 7.2 %backward.12 = (f32[2,2,128,128]{3,2,1,0:T(8,128)}, f32[2,2,128,128]{3,2,1,0:T(8,128)}, f32[2,2,128,128]{3,2,1,0:T(8,128)}, f32[2,128,1024]{2,1,0:T(8,128)}) custom-call(s32[2]{0:T(128)} %pad_add_fusion.3.refs_0_, bf16[2,128,1024]{2,1,0:T(8,128)(2,1)} %reshape.101.refs_1_, bf16[2,1024,128]{2,1,0:T(8,128)(2,1)} %bitcast.47, ...), custom_call_target="tpu_custom_call" | custom-call | flops 1006632960 | bytes 3145728 | tf_op jit(solution)/shard_map/backward/pallas_call | solution.py:202
  310.0 6.2 %collective-permute-done.33 = bf16[2,2,128,128]{3,2,1,0:T(8,128)(2,1)S(1)} collective-permute-done((bf16[2,2,128,128]{3,2,1,0:T(8,128)(2,1)S(1)}, bf16[2,2,128,128]{3,2,1,0:T(8,128)(2,1)S(1)}, u32[]{:S(2)}, u32[]{:S(2)}) %collective-permute-start.33) | collective-permute-done | bytes 131104 | tf_op jit(solution)/shard_map/ppermute | solution.py:307
  318.3 6.1 %collective-permute-done.34 = bf16[2,2,128,128]{3,2,1,0:T(8,128)(2,1)S(1)} collective-permute-done((bf16[2,2,128,128]{3,2,1,0:T(8,128)(2,1)S(1)}, bf16[2,2,128,128]{3,2,1,0:T(8,128)(2,1)S(1)}, u32[]{:S(2)}, u32[]{:S(2)}) %collective-permute-start.34) | collective-permute-done | bytes 131104 | tf_op jit(solution)/shard_map/ppermute | solution.py:307
  326.4 6.1 %backward.13 = (f32[2,2,128,128]{3,2,1,0:T(8,128)}, f32[2,2,128,128]{3,2,1,0:T(8,128)}, bf16[128,2048]{1,0:T(8,128)(2,1)}) custom-call(s32[2]{0:T(128)} %pad_add_fusion.3.refs_0_, bf16[2,128,1024]{2,1,0:T(8,128)(2,1)} %reshape.101.refs_1_, bf16[2,1024,128]{2,1,0:T(8,128)(2,1)} %bitcast.48, bf16[2,128,1024]{2,1,0:T(8,128)(2,1)} %reshape.103.refs_7_.refs_3_, ...), custom_call_target="tpu_custom_call" | custom-call | flops 671088640 | bytes 3145728 | tf_op jit(solution)/shard_map/backward/pallas_call | solution.py:202
  335.6 6.1 %collective-permute-done.36 = bf16[2,2,128,128]{3,2,1,0:T(8,128)(2,1)S(1)} collective-permute-done((bf16[2,2,128,128]{3,2,1,0:T(8,128)(2,1)S(1)}, bf16[2,2,128,128]{3,2,1,0:T(8,128)(2,1)S(1)}, u32[]{:S(2)}, u32[]{:S(2)}) %collective-permute-start.36) | collective-permute-done | bytes 131104 | tf_op jit(solution)/shard_map/ppermute | solution.py:307
  (178 shorter events, 172.5 us)
Async XLA Ops:
  2.9 8.2 %collective-permute-start.5 = (bf16[2,2,128,128]{3,2,1,0:T(8,128)(2,1)S(1)}, bf16[2,2,128,128]{3,2,1,0:T(8,128)(2,1)S(1)}, u32[]{:S(2)}, u32[]{:S(2)}) collective-permute-start(bf16[2,2,128,128]{3,2,1,0:T(8,128)(2,1)S(1)} %pad_maximum_fusion.refs_3_.refs_9_), channel_id=1, source_target_pairs={{0,2},{2,4},{4,6},{6,8},{8,10},{10,12},{12,14},{14,16},{16,18},{18... | collective-permute-start | bytes 393224 | tf_op jit(solution)/shard_map/ppermute | solution.py:270
  33.0 16.2 %collective-permute-start = (s32[1,4]{1,0:T(1,128)S(1)}, s32[1,4]{1,0:T(1,128)S(1)}, u32[]{:S(2)}, u32[]{:S(2)}) collective-permute-start(s32[1,4]{1,0:T(1,128)S(1)} %bitcast.82), channel_id=1, source_target_pairs={{0,2},{2,4},{4,6},{6,8},{8,10},{10,12},{12,14},{14,16},{16,18},{18... | collective-permute-start | bytes 56 | tf_op jit(solution)/shard_map/ppermute | solution.py:237
  43.5 18.3 %collective-permute-start.10 = (bf16[2,2,128,128]{3,2,1,0:T(8,128)(2,1)S(1)}, bf16[2,2,128,128]{3,2,1,0:T(8,128)(2,1)S(1)}, u32[]{:S(2)}, u32[]{:S(2)}) collective-permute-start(bf16[2,2,128,128]{3,2,1,0:T(8,128)(2,1)S(1)} %collective-permute-done.9.refs_3_.refs_10_), channel_id=1, source_target_pairs={{0,2},{2,4},{4,6},{6,8},{8,10},{10,12},{12,14},{14,16},{16,18},{18... | collective-permute-start | bytes 393224 | tf_op jit(solution)/shard_map/ppermute | solution.py:270
  53.8 12.3 %collective-permute-start.2 = (s32[4,4]{1,0:T(4,128)S(1)}, s32[4,4]{1,0:T(4,128)S(1)}, u32[]{:S(2)}, u32[]{:S(2)}) collective-permute-start(s32[4,4]{1,0:T(4,128)S(1)} %pad_add_fusion.1), channel_id=1, source_target_pairs={{0,8},{2,10},{4,12},{6,14},{8,16},{10,18},{12,20},{14,22},{16,24},... | collective-permute-start | bytes 200 | tf_op jit(solution)/shard_map/ppermute | solution.py:237
  61.9 39.1 %collective-permute-start.11 = (bf16[2,2,128,128]{3,2,1,0:T(8,128)(2,1)S(1)}, bf16[2,2,128,128]{3,2,1,0:T(8,128)(2,1)S(1)}, u32[]{:S(2)}, u32[]{:S(2)}) collective-permute-start(bf16[2,2,128,128]{3,2,1,0:T(8,128)(2,1)S(1)} %collective-permute-done.10.refs_4_.refs_9_), channel_id=1, source_target_pairs={{0,2},{2,4},{4,6},{6,8},{8,10},{10,12},{12,14},{14,16},{16,18},{18... | collective-permute-start | bytes 393224 | tf_op jit(solution)/shard_map/ppermute | solution.py:270
  66.1 12.4 %collective-permute-start.3 = (s32[8,4]{1,0:T(8,128)S(1)}, s32[8,4]{1,0:T(8,128)S(1)}, u32[]{:S(2)}, u32[]{:S(2)}) collective-permute-start(s32[8,4]{1,0:T(8,128)S(1)} %pad_add_fusion), channel_id=1, source_target_pairs={{0,16},{2,18},{4,20},{6,22},{8,24},{10,26},{12,28},{14,30},{16,32}... | collective-permute-start | bytes 392 | tf_op jit(solution)/shard_map/ppermute | solution.py:237
  78.7 22.0 %collective-permute-start.4 = (s32[16,4]{0,1:T(4,128)S(1)}, s32[16,4]{0,1:T(4,128)S(1)}, u32[]{:S(2)}, u32[]{:S(2)}) collective-permute-start(s32[16,4]{0,1:T(4,128)S(1)} %concatenate.22), channel_id=1, source_target_pairs={{0,32},{2,34},{4,36},{6,38},{8,40},{10,42},{12,44},{14,46},{16,48}... | collective-permute-start | bytes 776 | tf_op jit(solution)/shard_map/ppermute | solution.py:237
  101.0 8.1 %collective-permute-start.12 = (bf16[2,2,128,128]{3,2,1,0:T(8,128)(2,1)S(1)}, bf16[2,2,128,128]{3,2,1,0:T(8,128)(2,1)S(1)}, u32[]{:S(2)}, u32[]{:S(2)}) collective-permute-start(bf16[2,2,128,128]{3,2,1,0:T(8,128)(2,1)S(1)} %collective-permute-done.11.refs_5_.refs_8_), channel_id=1, source_target_pairs={{0,2},{2,4},{4,6},{6,8},{8,10},{10,12},{12,14},{14,16},{16,18},{18... | collective-permute-start | bytes 393224 | tf_op jit(solution)/shard_map/ppermute | solution.py:270
  125.4 9.3 %collective-permute-start.15 = (bf16[2,2,128,128]{3,2,1,0:T(8,128)(2,1)S(1)}, bf16[2,2,128,128]{3,2,1,0:T(8,128)(2,1)S(1)}, u32[]{:S(2)}, u32[]{:S(2)}) collective-permute-start(bf16[2,2,128,128]{3,2,1,0:T(8,128)(2,1)S(1)} %collective-permute-done.14.refs_4_.refs_8_), channel_id=1, source_target_pairs={{0,2},{2,4},{4,6},{6,8},{8,10},{10,12},{12,14},{14,16},{16,18},{18... | collective-permute-start | bytes 393224 | tf_op jit(solution)/shard_map/ppermute | solution.py:276
  134.7 8.6 %collective-permute-start.16 = (bf16[2,2,128,128]{3,2,1,0:T(8,128)(2,1)S(1)}, bf16[2,2,128,128]{3,2,1,0:T(8,128)(2,1)S(1)}, u32[]{:S(2)}, u32[]{:S(2)}) collective-permute-start(bf16[2,2,128,128]{3,2,1,0:T(8,128)(2,1)S(1)} %collective-permute-done.15.refs_5_.refs_10_), channel_id=1, source_target_pairs={{0,2},{2,4},{4,6},{6,8},{8,10},{10,12},{12,14},{14,16},{16,18},{18... | collective-permute-start | bytes 393224 | tf_op jit(solution)/shard_map/ppermute | solution.py:276
  151.4 11.7 %collective-permute-start.18 = (bf16[2,2,128,128]{3,2,1,0:T(8,128)(2,1)S(1)}, bf16[2,2,128,128]{3,2,1,0:T(8,128)(2,1)S(1)}, u32[]{:S(2)}, u32[]{:S(2)}) collective-permute-start(bf16[2,2,128,128]{3,2,1,0:T(8,128)(2,1)S(1)} %collective-permute-done.17.refs_3_.refs_8_), channel_id=1, source_target_pairs={{0,2},{2,4},{4,6},{6,8},{8,10},{10,12},{12,14},{14,16},{16,18},{18... | collective-permute-start | bytes 393224 | tf_op jit(solution)/shard_map/ppermute | solution.py:276
  163.2 11.1 %collective-permute-start.19 = (bf16[2,2,128,128]{3,2,1,0:T(8,128)(2,1)S(1)}, bf16[2,2,128,128]{3,2,1,0:T(8,128)(2,1)S(1)}, u32[]{:S(2)}, u32[]{:S(2)}) collective-permute-start(bf16[2,2,128,128]{3,2,1,0:T(8,128)(2,1)S(1)} %collective-permute-done.18.refs_4_.refs_9_), channel_id=1, source_target_pairs={{0,2},{2,4},{4,6},{6,8},{8,10},{10,12},{12,14},{14,16},{16,18},{18... | collective-permute-start | bytes 393224 | tf_op jit(solution)/shard_map/ppermute | solution.py:276
  174.2 14.5 %collective-permute-start.20 = (bf16[2,2,128,128]{3,2,1,0:T(8,128)(2,1)S(1)}, bf16[2,2,128,128]{3,2,1,0:T(8,128)(2,1)S(1)}, u32[]{:S(2)}, u32[]{:S(2)}) collective-permute-start(bf16[2,2,128,128]{3,2,1,0:T(8,128)(2,1)S(1)} %collective-permute-done.19.refs_5_.refs_8_), channel_id=1, source_target_pairs={{0,2},{2,4},{4,6},{6,8},{8,10},{10,12},{12,14},{14,16},{16,18},{18... | collective-permute-start | bytes 393224 | tf_op jit(solution)/shard_map/ppermute | solution.py:276
  196.7 9.1 %collective-permute-start.21 = (bf16[2,2,128,128]{3,2,1,0:T(8,128)(2,1)S(1)}, bf16[2,2,128,128]{3,2,1,0:T(8,128)(2,1)S(1)}, u32[]{:S(2)}, u32[]{:S(2)}) collective-permute-start(bf16[2,2,128,128]{3,2,1,0:T(8,128)(2,1)S(1)} %convert_element_type.106), channel_id=1, source_target_pairs={{2,0},{4,2},{6,4},{8,6},{10,8},{12,10},{14,12},{16,14},{18,16},{20... | collective-permute-start | bytes 393224 | tf_op jit(solution)/shard_map/ppermute | solution.py:307
  206.8 9.3 %collective-permute-start.22 = (bf16[2,2,128,128]{3,2,1,0:T(8,128)(2,1)S(1)}, bf16[2,2,128,128]{3,2,1,0:T(8,128)(2,1)S(1)}, u32[]{:S(2)}, u32[]{:S(2)}) collective-permute-start(bf16[2,2,128,128]{3,2,1,0:T(8,128)(2,1)S(1)} %add_convert_fusion.14), channel_id=1, source_target_pairs={{2,0},{4,2},{6,4},{8,6},{10,8},{12,10},{14,12},{16,14},{18,16},{20... | collective-permute-start | bytes 393224 | tf_op jit(solution)/shard_map/ppermute | solution.py:307
  225.3 8.7 %collective-permute-start.24 = (bf16[2,2,128,128]{3,2,1,0:T(8,128)(2,1)S(1)}, bf16[2,2,128,128]{3,2,1,0:T(8,128)(2,1)S(1)}, u32[]{:S(2)}, u32[]{:S(2)}) collective-permute-start(bf16[2,2,128,128]{3,2,1,0:T(8,128)(2,1)S(1)} %add_convert_fusion.12), channel_id=1, source_target_pairs={{2,0},{4,2},{6,4},{8,6},{10,8},{12,10},{14,12},{16,14},{18,16},{20... | collective-permute-start | bytes 393224 | tf_op jit(solution)/shard_map/ppermute | solution.py:307
  234.1 9.3 %collective-permute-start.25 = (bf16[2,2,128,128]{3,2,1,0:T(8,128)(2,1)S(1)}, bf16[2,2,128,128]{3,2,1,0:T(8,128)(2,1)S(1)}, u32[]{:S(2)}, u32[]{:S(2)}) collective-permute-start(bf16[2,2,128,128]{3,2,1,0:T(8,128)(2,1)S(1)} %add_convert_fusion.11), channel_id=1, source_target_pairs={{2,0},{4,2},{6,4},{8,6},{10,8},{12,10},{14,12},{16,14},{18,16},{20... | collective-permute-start | bytes 393224 | tf_op jit(solution)/shard_map/ppermute | solution.py:307
  243.4 8.3 %collective-permute-start.26 = (bf16[2,2,128,128]{3,2,1,0:T(8,128)(2,1)S(1)}, bf16[2,2,128,128]{3,2,1,0:T(8,128)(2,1)S(1)}, u32[]{:S(2)}, u32[]{:S(2)}) collective-permute-start(bf16[2,2,128,128]{3,2,1,0:T(8,128)(2,1)S(1)} %add_convert_fusion.10), channel_id=1, source_target_pairs={{2,0},{4,2},{6,4},{8,6},{10,8},{12,10},{14,12},{16,14},{18,16},{20... | collective-permute-start | bytes 393224 | tf_op jit(solution)/shard_map/ppermute | solution.py:307
  252.7 9.4 %collective-permute-start.27 = (bf16[2,2,128,128]{3,2,1,0:T(8,128)(2,1)S(1)}, bf16[2,2,128,128]{3,2,1,0:T(8,128)(2,1)S(1)}, u32[]{:S(2)}, u32[]{:S(2)}) collective-permute-start(bf16[2,2,128,128]{3,2,1,0:T(8,128)(2,1)S(1)} %add_convert_fusion.9), channel_id=1, source_target_pairs={{2,0},{4,2},{6,4},{8,6},{10,8},{12,10},{14,12},{16,14},{18,16},{20... | collective-permute-start | bytes 393224 | tf_op jit(solution)/shard_map/ppermute | solution.py:307
  262.2 8.7 %collective-permute-start.28 = (bf16[2,2,128,128]{3,2,1,0:T(8,128)(2,1)S(1)}, bf16[2,2,128,128]{3,2,1,0:T(8,128)(2,1)S(1)}, u32[]{:S(2)}, u32[]{:S(2)}) collective-permute-start(bf16[2,2,128,128]{3,2,1,0:T(8,128)(2,1)S(1)} %add_convert_fusion.8), channel_id=1, source_target_pairs={{2,0},{4,2},{6,4},{8,6},{10,8},{12,10},{14,12},{16,14},{18,16},{20... | collective-permute-start | bytes 393224 | tf_op jit(solution)/shard_map/ppermute | solution.py:307
  270.9 9.4 %collective-permute-start.29 = (bf16[2,2,128,128]{3,2,1,0:T(8,128)(2,1)S(1)}, bf16[2,2,128,128]{3,2,1,0:T(8,128)(2,1)S(1)}, u32[]{:S(2)}, u32[]{:S(2)}) collective-permute-start(bf16[2,2,128,128]{3,2,1,0:T(8,128)(2,1)S(1)} %add_convert_fusion.7), channel_id=1, source_target_pairs={{2,0},{4,2},{6,4},{8,6},{10,8},{12,10},{14,12},{16,14},{18,16},{20... | collective-permute-start | bytes 393224 | tf_op jit(solution)/shard_map/ppermute | solution.py:307
  289.5 8.2 %collective-permute-start.31 = (bf16[2,2,128,128]{3,2,1,0:T(8,128)(2,1)S(1)}, bf16[2,2,128,128]{3,2,1,0:T(8,128)(2,1)S(1)}, u32[]{:S(2)}, u32[]{:S(2)}) collective-permute-start(bf16[2,2,128,128]{3,2,1,0:T(8,128)(2,1)S(1)} %add_convert_fusion.5), channel_id=1, source_target_pairs={{2,0},{4,2},{6,4},{8,6},{10,8},{12,10},{14,12},{16,14},{18,16},{20... | collective-permute-start | bytes 393224 | tf_op jit(solution)/shard_map/ppermute | solution.py:307
  297.8 9.2 %collective-permute-start.32 = (bf16[2,2,128,128]{3,2,1,0:T(8,128)(2,1)S(1)}, bf16[2,2,128,128]{3,2,1,0:T(8,128)(2,1)S(1)}, u32[]{:S(2)}, u32[]{:S(2)}) collective-permute-start(bf16[2,2,128,128]{3,2,1,0:T(8,128)(2,1)S(1)} %add_convert_fusion.4), channel_id=1, source_target_pairs={{2,0},{4,2},{6,4},{8,6},{10,8},{12,10},{14,12},{16,14},{18,16},{20... | collective-permute-start | bytes 393224 | tf_op jit(solution)/shard_map/ppermute | solution.py:307
  316.2 8.2 %collective-permute-start.34 = (bf16[2,2,128,128]{3,2,1,0:T(8,128)(2,1)S(1)}, bf16[2,2,128,128]{3,2,1,0:T(8,128)(2,1)S(1)}, u32[]{:S(2)}, u32[]{:S(2)}) collective-permute-start(bf16[2,2,128,128]{3,2,1,0:T(8,128)(2,1)S(1)} %add_convert_fusion.2), channel_id=1, source_target_pairs={{2,0},{4,2},{6,4},{8,6},{10,8},{12,10},{14,12},{16,14},{18,16},{20... | collective-permute-start | bytes 393224 | tf_op jit(solution)/shard_map/ppermute | solution.py:307
  (43 other events, 1519.2 us)
